TPU v7x, 32 devices: a whole 2x2x4 slice. The times are simulated.
32 devices in a mesh: section: 4 (over y, x), owner: 8 (over z, core).
Axes of the slice: x: 2, y: 2, z: 4, core: 2. Of those that a mesh axis runs over, the one named last changes fastest.
Arguments:
- weights: bfloat16 [4, 1024, 1024], P('section'), may hold values from -0.1875 to 0.1875
- inputs: bfloat16 [4, 4, 2048, 1024], P('section', None, 'owner'), may hold values from -6 to 6
- preact: bfloat16 [4, 4, 2048, 1024], P('section', None, 'owner'), may hold values from -6 to 6
- cotangent: bfloat16 [4, 2048, 1024], P(None, 'owner'), may hold values from -6 to 6
- embeddings: bfloat16 [4, 2048, 32, 128], P(None, ('owner', 'section')), may hold values from -6 to 6
- row_ids: int32 [4, 2048, 32], P(None, ('owner', 'section')), may hold values from 0 to 511
Outputs:
- weight_grad: float32 [4, 1024, 1024], P('section', 'owner')
- table_grad: float32 [32, 512, 128], P('owner', 'section')
All inputs are finite; a program needn't handle non-finite values.
Results may differ from a plain program's by a relative error of at most 0.0064.
Values may be sent and summed in bfloat16 or wider, within the bound.
A program may use at most 128 MiB of HBM per device.

v0:
```python
import functools
import math

import jax
import jax.numpy as jnp
from jax import lax
from jax.experimental import pallas as pl
from jax.experimental.pallas import tpu as pltpu
from jax.sharding import PartitionSpec as P

TROWS = 512
PIECE = 16
SPAN = 512


def exclusive_or(a, b, bits):
    total = 0
    for k in range(bits):
        total = total + lax.rem(a // (1 << k) + b // (1 << k), 2) * (1 << k)
    return total


def step_kernel(
    dims, w_hbm, pre_hbm, cot_hbm, in_hbm, emb_hbm, ids_ref, wg_ref, table_ref,
    w, pre, cot, inp, emb, slope, in_buf, out_buf, portion, square, pairs, outgoing, arrived,
    places, ids, acc, wsend, wrecv, tacc, tsend, trecv,
    w_sem, pre_sem, cot_sem, inp_sem, emb_sem, out_sem, in_sem, portion_sem, send_sem, recv_sem,
    ids_send, ids_recv, wsend_sem, wrecv_sem, tsend_sem, trecv_sem,
):
    sections, owners, micro_count, quarter, features, width, slots, row_split, grad_scale = dims
    section = lax.axis_index("section")
    owner = lax.axis_index("owner")
    last = sections - 1
    lane_groups = 128 // features
    hidden = w.shape[0]
    per_micro = quarter // PIECE
    chunks = micro_count * per_micro
    chunk_rows = sections * PIECE
    bits = owners.bit_length() - 1
    block = hidden // owners
    share = TROWS // sections

    barrier = pltpu.get_barrier_semaphore()
    for k in range(1, owners):
        pl.semaphore_signal(
            barrier, inc=1, device_id={"owner": lax.rem(owner + k, owners)},
            device_id_type=pl.DeviceIdType.MESH,
        )
    for k in range(1, sections):
        pl.semaphore_signal(
            barrier, inc=1, device_id={"section": lax.rem(section + k, sections)},
            device_id_type=pl.DeviceIdType.MESH,
        )

    def load_w():
        return pltpu.make_async_copy(w_hbm, w, w_sem)

    def load_pre(m):
        return pltpu.make_async_copy(pre_hbm.at[m], pre.at[m], pre_sem.at[m])

    def load_cot(m):
        return pltpu.make_async_copy(cot_hbm.at[m], cot.at[m], cot_sem.at[m])

    def load_inp():
        return pltpu.make_async_copy(in_hbm, inp, inp_sem)

    def load_emb():
        return pltpu.make_async_copy(emb_hbm, emb, emb_sem)

    load_w().start()
    for m in range(micro_count):
        load_pre(m).start()

        @pl.when(section == last)
        def _():
            load_cot(m).start()

    load_emb().start()
    load_inp().start()
    acc[...] = jnp.zeros_like(acc)
    tacc[...] = jnp.zeros_like(tacc)

    def along(c):
        return pltpu.make_async_remote_copy(
            src_ref=out_buf.at[c], dst_ref=in_buf.at[c],
            send_sem=out_sem.at[c], recv_sem=in_sem.at[c],
            device_id={"section": lax.rem(section + last, sections)},
            device_id_type=pl.DeviceIdType.MESH,
        )

    def hand(c, target):
        return pltpu.make_async_remote_copy(
            src_ref=out_buf.at[c, pl.ds(target * PIECE, PIECE)], dst_ref=portion.at[c],
            send_sem=out_sem.at[c], recv_sem=portion_sem.at[c],
            device_id={"section": target},
            device_id_type=pl.DeviceIdType.MESH,
        )

    def landing(m, j, source):
        return arrived.at[m, source, pl.ds(pl.multiple_of(j * PIECE, PIECE), PIECE)]

    def exchange(c, target):
        return pltpu.make_async_remote_copy(
            src_ref=outgoing.at[target, c],
            dst_ref=landing(c // per_micro, lax.rem(c, per_micro), owner),
            send_sem=send_sem.at[target], recv_sem=recv_sem.at[c],
            device_id={"owner": target},
            device_id_type=pl.DeviceIdType.MESH,
        )

    def exchange_own(c):
        return pltpu.make_async_copy(
            outgoing.at[owner, c],
            landing(c // per_micro, lax.rem(c, per_micro), owner), recv_sem.at[c],
        )

    def exchange_ids(target):
        return pltpu.make_async_remote_copy(
            src_ref=ids_ref.at[target], dst_ref=places.at[owner],
            send_sem=ids_send.at[target], recv_sem=ids_recv,
            device_id={"owner": target},
            device_id_type=pl.DeviceIdType.MESH,
        )

    def reduce_copy(d, k):
        return pltpu.make_async_remote_copy(
            src_ref=wsend.at[d], dst_ref=wrecv.at[d],
            send_sem=wsend_sem.at[d], recv_sem=wrecv_sem.at[d],
            device_id={"owner": exclusive_or(owner, 1 << k, bits)},
            device_id_type=pl.DeviceIdType.MESH,
        )

    def share_copy(target):
        return pltpu.make_async_remote_copy(
            src_ref=tsend.at[target], dst_ref=trecv.at[section],
            send_sem=tsend_sem.at[target], recv_sem=trecv_sem.at[section],
            device_id={"section": target},
            device_id_type=pl.DeviceIdType.MESH,
        )

    def chain(c):
        m, j = c // per_micro, lax.rem(c, per_micro)
        rows = pl.ds(pl.multiple_of(j * PIECE, PIECE), PIECE)

        @pl.when(j == 0)
        def _():
            load_pre(m).wait()

            @pl.when(section == last)
            def _():
                load_cot(m).wait()

        positive = pre[m, :, rows, :].astype(jnp.float32) > 0

        def masked(incoming):
            grad = incoming.astype(jnp.float32)
            slope[m, :, rows, :] = jnp.where(positive, grad, 0.0).astype(jnp.bfloat16)

        @pl.when(section == last)
        def _():
            masked(cot[m, :, rows, :])

        @pl.when(section < last)
        def _():
            along(c).wait_recv()
            masked(in_buf[c].reshape(sections, PIECE, hidden))

        out_buf[c] = lax.dot_general(
            slope[m, :, rows, :].reshape(chunk_rows, hidden), w[...], (((1,), (1,)), ((), ())),
            preferred_element_type=jnp.float32,
        ).astype(jnp.bfloat16)

        @pl.when(section > 0)
        def _():
            along(c).start()

        @pl.when(section == 0)
        def _():
            for target in range(1, sections):
                hand(c, target).start()
            portion[c] = out_buf[c, :PIECE]

    def pair(c):
        m, j = c // per_micro, lax.rem(c, per_micro)

        @pl.when(section > 0)
        def _():
            hand(c, 0).wait_recv()

        for f in range(features):
            group, part = f // lane_groups, f % lane_groups
            piece = portion[c, :, group * 128 : (group + 1) * 128].astype(jnp.float32)
            if part:
                piece = pltpu.roll(piece, 128 - part * features, 1)
            square[pl.ds(f, PIECE, stride=features), :] = piece
        whole = square[...].reshape(PIECE, features, 128)[:, :, :features]
        both = (whole + jnp.swapaxes(whole, 1, 2)).astype(jnp.bfloat16)
        rows = pl.ds(pl.multiple_of(j * PIECE, PIECE), PIECE)
        pairs[...] = lax.dot_general(
            both, emb[m, rows], (((2,), (1,)), ((0,), (0,))),
            preferred_element_type=jnp.float32,
        ).reshape(PIECE * features, width)
        for target in range(owners):
            for slot in range(slots):
                f = (target * slots + slot) // row_split
                outgoing[target, c, :, slot * width : (slot + 1) * width] = pairs[
                    pl.ds(f, PIECE, stride=features), :
                ].astype(jnp.bfloat16)

        def send(k, carry):
            exchange(c, lax.rem(owner + k, owners)).start()
            return carry

        lax.fori_loop(1, owners, send, 0)
        exchange_own(c).start()

    def weigh(m):
        acc[...] += lax.dot_general(
            inp[m], slope[m].reshape(sections * quarter, hidden), (((0,), (0,)), ((), ())),
            preferred_element_type=jnp.float32,
        )

    def block_of(d):
        at = exclusive_or(owner, d, bits) * block
        return pl.ds(pl.multiple_of(at, block), block)

    def send_block(d, k):
        wsend[d] = acc[block_of(d), :].astype(jnp.bfloat16)
        reduce_copy(d, k).start()

    def reduce_stage(k):
        held = owners >> k

        def one(i, carry):
            h = held - 1 - i
            if k > 0:
                d = (1 << (k - 1)) + h * (1 << k)
                reduce_copy(d, k - 1).wait_recv()
                at = block_of(h * (1 << k))
                acc[at, :] = acc[at, :] + wrecv[d].astype(jnp.float32)
            if k < bits:
                @pl.when(lax.rem(h, 2) == 1)
                def _():
                    send_block(h * (1 << k), k)

            return carry

        lax.fori_loop(0, held, one, 0)

    def gather_ids():
        pltpu.make_async_copy(places, places, ids_recv).wait()
        for m in range(micro_count):
            for source in range(owners):
                ids[m, :, source * quarter : (source + 1) * quarter] = places[
                    source, :, m * quarter : (m + 1) * quarter
                ]

    span = min(SPAN, owners * quarter)

    def tabulate(m):
        for j in range(per_micro):
            batch = arrived.at[m, :, pl.ds(j * PIECE, PIECE)]
            pltpu.make_async_copy(batch, batch, recv_sem.at[m * per_micro + j]).wait()

        def one(b, carry):
            sources = span // quarter
            rows = arrived[m, pl.ds(b * sources, sources)].reshape(span, slots * width)
            for slot in range(slots):
                row_block = lax.rem(owner * slots + slot, row_split)
                here = ids[m, slot : slot + 1, pl.ds(pl.multiple_of(b * span, span), span)]
                positions = lax.broadcasted_iota(jnp.int32, (TROWS, span), 0)
                onehot = (positions == here - row_block * TROWS).astype(jnp.float32)
                tacc[slot] += lax.dot_general(
                    onehot.astype(jnp.bfloat16), rows[:, slot * width : (slot + 1) * width],
                    (((1,), (0,)), ((), ())), preferred_element_type=jnp.float32,
                )
            return carry

        lax.fori_loop(0, owners * quarter // span, one, 0)

    def share_tables():
        for target in range(sections):
            @pl.when(section != target)
            def _():
                tsend[target] = tacc[:, target * share : (target + 1) * share, :].astype(jnp.bfloat16)
                share_copy(target).start()

    pl.semaphore_wait(barrier, owners - 1 + sections - 1)

    own_ids = pltpu.make_async_copy(ids_ref.at[owner], places.at[owner], ids_recv)
    own_ids.start()

    def send_ids(k, carry):
        exchange_ids(lax.rem(owner + k, owners)).start()
        return carry

    lax.fori_loop(1, owners, send_ids, 0)
    load_w().wait()

    lag = jnp.where(
        section == last, chunks, jnp.where(section == 0, 0, section * 2 + 2)
    )
    stage_ticks = [chunks - 1, chunks] + [chunks + 6 + 2 * i for i in range(bits - 1)]
    ticks = max(chunks + chunks + 2, stage_ticks[-1] + 1)

    def step(t, carry):
        @pl.when(t < chunks)
        def _():
            chain(t)

            @pl.when(lax.rem(t, per_micro) == per_micro - 1)
            def _():
                m = t // per_micro

                @pl.when(m == 0)
                def _():
                    load_inp().wait()

                weigh(m)

        p = t - lag

        @pl.when((p >= 0) & (p < chunks))
        def _():
            @pl.when(p == 0)
            def _():
                load_emb().wait()

            pair(p)

        for k in range(bits + 1):
            @pl.when(t == stage_ticks[k])
            def _():
                reduce_stage(k)

        @pl.when(p == per_micro)
        def _():
            gather_ids()

        @pl.when((p > per_micro) & (lax.rem(p, per_micro) == 1) & (p < chunks + per_micro))
        def _():
            tabulate(p // per_micro - 1)

        @pl.when(p == chunks + 1)
        def _():
            share_tables()

        return carry

    lax.fori_loop(0, ticks, step, 0)

    wg_ref[...] = acc[block_of(0), :] * grad_scale

    mine = pl.ds(pl.multiple_of(section * share, share), share)
    total = tacc[:, mine, :]
    for k in range(1, sections):
        source = lax.rem(section + k, sections)
        pltpu.make_async_copy(trecv.at[source], trecv.at[source], trecv_sem.at[source]).wait()
        total = total + trecv[source].astype(jnp.float32)
    table_ref[...] = total * grad_scale

    def drain_chain(c, carry):
        @pl.when(section > 0)
        def _():
            along(c).wait_send()

        @pl.when(section == 0)
        def _():
            sent = out_buf.at[c, pl.ds(0, (sections - 1) * PIECE)]
            pltpu.make_async_copy(sent, sent, out_sem.at[c]).wait()

        return carry

    lax.fori_loop(0, chunks, drain_chain, 0)

    def drain_exchange(k, carry):
        target = lax.rem(owner + k, owners)
        sent = outgoing.at[target]
        pltpu.make_async_copy(sent, sent, send_sem.at[target]).wait()
        exchange_ids(target).wait_send()
        reduce_copy(k, 0).wait_send()
        return carry

    lax.fori_loop(1, owners, drain_exchange, 0)
    for k in range(1, sections):
        share_copy(lax.rem(section + k, sections)).wait_send()


def whole_step(layer_w, layer_pre, cotangent, layer_in, embeddings, ids_out, row_split, scale):
    sections = lax.axis_size("section")
    owners = lax.axis_size("owner")
    micro_count, batch_rows, hidden = cotangent.shape
    quarter, features, width = embeddings.shape[1:]
    slots = ids_out.shape[1]
    chunks = micro_count * (quarter // PIECE)
    share = TROWS // sections
    dims = (sections, owners, micro_count, quarter, features, width, slots, row_split, scale)
    vmem = pl.BlockSpec(memory_space=pltpu.VMEM)
    anywhere = pl.BlockSpec(memory_space=pl.ANY)
    narrow, wide, whole = jnp.bfloat16, jnp.float32, jnp.int32
    split = (micro_count, sections, quarter, hidden)
    chunk_shape = (chunks, sections * PIECE, hidden)
    dma = pltpu.SemaphoreType.DMA
    return pl.pallas_call(
        functools.partial(step_kernel, dims),
        out_shape=(
            jax.ShapeDtypeStruct((hidden // owners, hidden), wide),
            jax.ShapeDtypeStruct((slots, share, width), wide),
        ),
        in_specs=[anywhere] * 5 + [vmem],
        out_specs=(vmem, vmem),
        scratch_shapes=[
            pltpu.VMEM((hidden, hidden), narrow),
            pltpu.VMEM(split, narrow),
            pltpu.VMEM(split, narrow),
            pltpu.VMEM((micro_count, batch_rows, hidden), narrow),
            pltpu.VMEM(embeddings.shape, narrow),
            pltpu.VMEM(split, narrow),
            pltpu.VMEM(chunk_shape, narrow),
            pltpu.VMEM(chunk_shape, narrow),
            pltpu.VMEM((chunks, PIECE, hidden), narrow),
            pltpu.VMEM((PIECE * features, 128), wide),
            pltpu.VMEM((PIECE * features, width), wide),
            pltpu.VMEM((owners, chunks, PIECE, slots * width), narrow),
            pltpu.VMEM((micro_count, owners, quarter, slots * width), narrow),
            pltpu.VMEM(ids_out.shape, whole),
            pltpu.VMEM((micro_count, slots, owners * quarter), whole),
            pltpu.VMEM((hidden, hidden), wide),
            pltpu.VMEM((owners, hidden // owners, hidden), narrow),
            pltpu.VMEM((owners, hidden // owners, hidden), narrow),
            pltpu.VMEM((slots, TROWS, width), wide),
            pltpu.VMEM((sections, slots, share, width), narrow),
            pltpu.VMEM((sections, slots, share, width), narrow),
            dma(()),
            dma((micro_count,)),
            dma((micro_count,)),
            dma(()),
            dma(()),
            dma((chunks,)),
            dma((chunks,)),
            dma((chunks,)),
            dma((owners,)),
            dma((chunks,)),
            dma((owners,)),
            dma(()),
            dma((owners,)),
            dma((owners,)),
            dma((sections,)),
            dma((sections,)),
        ],
        compiler_params=pltpu.CompilerParams(
            collective_id=0, has_side_effects=True, vmem_limit_bytes=56 * 1024 * 1024
        ),
    )(
        layer_w, layer_pre.reshape(split), cotangent.reshape(split), layer_in, embeddings, ids_out
    )


def per_device(weights, inputs, preact, cotangent, embeddings, row_ids):
    owners = lax.axis_size("owner")
    micro_count, batch_rows, hidden = cotangent.shape
    quarter, features, width = embeddings.shape[1:]
    row_split = max(1, owners // features)
    slots = features * row_split // owners
    grad_scale = 1.0 / math.sqrt(micro_count * batch_rows * owners)
    ids_out = jnp.repeat(
        row_ids.reshape(micro_count * quarter, features).T, row_split, axis=0
    ).reshape(owners, slots, micro_count * quarter)
    weight_grad, table_grad = whole_step(
        weights[0], preact[0], cotangent, inputs[0], embeddings, ids_out, row_split, grad_scale
    )
    return (weight_grad[None], table_grad)


def solution(mesh):
    return jax.shard_map(
        per_device,
        mesh=mesh,
        in_specs=(
            P("section", None, None),
            P("section", None, "owner", None),
            P("section", None, "owner", None),
            P(None, "owner", None),
            P(None, ("owner", "section"), None, None),
            P(None, ("owner", "section"), None),
        ),
        out_specs=(P("section", "owner", None), P("owner", "section", None)),
        check_vma=False,
    )
```

profile of v0, /device:TPU:2, one launch (start us, length us, event | category | flops | bytes accessed | tf_op | source)
XLA Modules:
  0.0 107.2 jit_solution(6063898402363819468)
XLA Ops:
  0.6 0.9 copy.8
  1.5 0.1 reshape.11
  1.6 0.6 reshape_reshape_broadcast_in_dim.3.ids_ref
  2.3 101.3 %shard_map.77 = (f32[128,1024]{1,0:T(8,128)}, f32[4,128,128]{2,1,0:T(8,128)}) custom-call(bf16[1024,1024]{1,0:T(8,128)(2,1)} %bitcast.8, bf16[4,4,64,1024]{3,2,1,0:T(8,128)(2,1)} %bitcast.9, bf16[4,4,64,1024]{3,2,1,0:T(8,128)(2,1)} %bitcast.10, bf16[4,256,1024]{2,1,0:T(8,128)(2,1)} %bitcast.11, bf16[4,64,32,128]{3,2,1,0:T(8,128)(2,1)} %emb_hbm.1, ...), custom_call_target="tpu_custom_call" | custom-call | tf_op jit(solution)/shard_map/pallas_call | solution.py:404
  103.6 1.9 %copy.11 = f32[1,128,1024]{2,1,0:T(8,128)} copy(f32[1,128,1024]{2,1,0:T(8,128)} %bitcast.12) | data formatting | bytes 1048576
  105.5 1.7 %copy.12 = f32[4,128,128]{2,1,0:T(8,128)} copy(f32[4,128,128]{2,1,0:T(8,128)} %get-tuple-element.9) | data formatting | bytes 524288
where the time goes:
time: 107 us
  Pallas kernels  101 us (94%)
  local copies, waits for them, and re-layouts  5.17 us (5%)
    pallas_call x1, Pallas kernels, whole_step(): pl.pallas_call(functools.partial(step_kernel, dims), out_shape=(jax.Shape...  101 us
    unnamed x3, local copies, waits for them, and re-layouts  4.44 us

commit v1 on v0

v1 whole, which is shorter than its diff:
```python
import functools
import math

import jax
import jax.numpy as jnp
from jax import lax
from jax.experimental import pallas as pl
from jax.experimental.pallas import tpu as pltpu
from jax.sharding import PartitionSpec as P

TROWS = 512
PIECE = 16
SPAN = 512
GROUP = 2


def exclusive_or(a, b, bits):
    total = 0
    for k in range(bits):
        total = total + lax.rem(a // (1 << k) + b // (1 << k), 2) * (1 << k)
    return total


def step_kernel(
    dims, w_hbm, pre_hbm, cot_hbm, in_hbm, emb_hbm, ids_hbm, wg_ref, table_ref,
    w, wt, pre, cot, inp, emb, raw, slope, in_buf, out_buf, portion, square, pairs, outgoing,
    arrived, mine, places, ids, acc, wsend, wrecv, tacc, tsend, trecv,
    w_sem, pre_sem, cot_sem, inp_sem, emb_sem, raw_sem, out_sem, in_sem, hand_sem, portion_sem,
    send_sem, recv_sem, ids_send, ids_recv, wsend_sem, wrecv_sem, tsend_sem, trecv_sem,
):
    sections, owners, micro_count, quarter, features, width, slots, row_split = dims
    section = lax.axis_index("section")
    owner = lax.axis_index("owner")
    last = sections - 1
    lane_groups = 128 // features
    hidden = w.shape[0]
    per_micro = quarter // PIECE
    chunks = micro_count * per_micro
    subs = sections // GROUP
    bits = owners.bit_length() - 1
    block = hidden // owners
    share = TROWS // sections

    barrier = pltpu.get_barrier_semaphore()
    for k in range(1, sections):
        pl.semaphore_signal(
            barrier, inc=1, device_id={"section": lax.rem(section + k, sections)},
            device_id_type=pl.DeviceIdType.MESH,
        )
    for k in range(1, owners):
        pl.semaphore_signal(
            barrier, inc=1, device_id={"owner": lax.rem(owner + k, owners)},
            device_id_type=pl.DeviceIdType.MESH,
        )

    def load_w():
        return pltpu.make_async_copy(w_hbm, w, w_sem)

    def load_pre(m):
        return pltpu.make_async_copy(pre_hbm.at[m], pre.at[m], pre_sem.at[m])

    def load_cot(m):
        return pltpu.make_async_copy(cot_hbm.at[m], cot.at[m], cot_sem.at[m])

    def load_inp():
        return pltpu.make_async_copy(in_hbm, inp, inp_sem)

    def load_emb():
        return pltpu.make_async_copy(emb_hbm, emb, emb_sem)

    def load_raw():
        return pltpu.make_async_copy(ids_hbm, raw, raw_sem)

    load_w().start()
    for m in range(micro_count):
        load_pre(m).start()

        @pl.when(section == last)
        def _():
            load_cot(m).start()

    load_raw().start()
    load_emb().start()
    load_inp().start()

    def rows_of(j):
        return pl.ds(pl.multiple_of(j * PIECE, PIECE), PIECE)

    def place(u):
        c = u // subs
        base = (subs - 1 - lax.rem(u, subs)) * GROUP
        return c // per_micro, pl.ds(base, GROUP), rows_of(lax.rem(c, per_micro))

    def along(u):
        at = place(u)
        return pltpu.make_async_remote_copy(
            src_ref=out_buf.at[at], dst_ref=in_buf.at[at],
            send_sem=out_sem.at[u], recv_sem=in_sem.at[u],
            device_id={"section": lax.rem(section + last, sections)},
            device_id_type=pl.DeviceIdType.MESH,
        )

    def hand(c, target):
        return pltpu.make_async_remote_copy(
            src_ref=out_buf.at[c // per_micro, target, rows_of(lax.rem(c, per_micro))],
            dst_ref=portion.at[c],
            send_sem=hand_sem.at[c], recv_sem=portion_sem.at[c],
            device_id={"section": target},
            device_id_type=pl.DeviceIdType.MESH,
        )

    def landing(c):
        return arrived.at[c // per_micro, owner, rows_of(lax.rem(c, per_micro))]

    def exchange(c, target):
        return pltpu.make_async_remote_copy(
            src_ref=outgoing.at[target, c], dst_ref=landing(c),
            send_sem=send_sem.at[target], recv_sem=recv_sem.at[c],
            device_id={"owner": target},
            device_id_type=pl.DeviceIdType.MESH,
        )

    def exchange_ids(target):
        return pltpu.make_async_remote_copy(
            src_ref=mine.at[target], dst_ref=places.at[owner],
            send_sem=ids_send.at[target], recv_sem=ids_recv,
            device_id={"owner": target},
            device_id_type=pl.DeviceIdType.MESH,
        )

    def reduce_copy(d, k):
        return pltpu.make_async_remote_copy(
            src_ref=wsend.at[d], dst_ref=wrecv.at[d],
            send_sem=wsend_sem.at[d], recv_sem=wrecv_sem.at[d],
            device_id={"owner": exclusive_or(owner, 1 << k, bits)},
            device_id_type=pl.DeviceIdType.MESH,
        )

    def share_copy(target):
        return pltpu.make_async_remote_copy(
            src_ref=tsend.at[target], dst_ref=trecv.at[section],
            send_sem=tsend_sem.at[target], recv_sem=trecv_sem.at[section],
            device_id={"section": target},
            device_id_type=pl.DeviceIdType.MESH,
        )

    def head(m):
        load_pre(m).wait()
        load_cot(m).wait()
        positive = pre[m].astype(jnp.float32) > 0
        slope[m] = jnp.where(positive, cot[m].astype(jnp.float32), 0.0).astype(jnp.bfloat16)
        out_buf[m] = lax.dot_general(
            slope[m].reshape(sections * quarter, hidden), w[...], (((1,), (1,)), ((), ())),
            preferred_element_type=jnp.float32,
        ).astype(jnp.bfloat16).reshape(sections, quarter, hidden)

        def send(i, carry):
            along(m * per_micro * subs + i).start()
            return carry

        lax.fori_loop(0, per_micro * subs, send, 0)

    def chain(c, i):
        u = c * subs + i
        m, j = c // per_micro, lax.rem(c, per_micro)
        base = (subs - 1 - i) * GROUP
        at = (m, pl.ds(base, GROUP), rows_of(j))
        positive = pre[at].astype(jnp.float32) > 0
        with jax.named_scope("arrive"):
            along(u).wait_recv()
        grad = in_buf[at].astype(jnp.float32)
        slope[at] = jnp.where(positive, grad, 0.0).astype(jnp.bfloat16)
        out_buf[at] = lax.dot_general(
            slope[at].reshape(GROUP * PIECE, hidden), wt[...], (((1,), (0,)), ((), ())),
            preferred_element_type=jnp.float32,
        ).astype(jnp.bfloat16).reshape(GROUP, PIECE, hidden)

        @pl.when(section > 0)
        def _():
            along(u).start()

        @pl.when(section == 0)
        def _():
            for target in range(base, base + GROUP):
                if target == 0:
                    portion[c] = out_buf[m, 0, rows_of(j)]
                else:
                    hand(c, target).start()

    def pair(c):
        m, j = c // per_micro, lax.rem(c, per_micro)

        @pl.when(section > 0)
        def _():
            with jax.named_scope("handed"):
                hand(c, 0).wait_recv()

        for f in range(features):
            group, part = f // lane_groups, f % lane_groups
            piece = portion[c, :, group * 128 : (group + 1) * 128].astype(jnp.float32)
            if part:
                piece = pltpu.roll(piece, 128 - part * features, 1)
            square[pl.ds(f, PIECE, stride=features), :] = piece
        whole = square[...].reshape(PIECE, features, 128)[:, :, :features]
        both = (whole + jnp.swapaxes(whole, 1, 2)).astype(jnp.bfloat16)
        pairs[...] = lax.dot_general(
            both, emb[m, rows_of(j)], (((2,), (1,)), ((0,), (0,))),
            preferred_element_type=jnp.float32,
        ).reshape(PIECE * features, width)
        for target in range(owners):
            for slot in range(slots):
                f = (target * slots + slot) // row_split
                outgoing[target, c, :, slot * width : (slot + 1) * width] = pairs[
                    pl.ds(f, PIECE, stride=features), :
                ].astype(jnp.bfloat16)

        def send(k, carry):
            exchange(c, lax.rem(owner + k, owners)).start()
            return carry

        lax.fori_loop(1, owners, send, 0)
        pltpu.make_async_copy(outgoing.at[owner, c], landing(c), recv_sem.at[c]).start()

    def weigh(m):
        def product():
            return lax.dot_general(
                inp[m], slope[m].reshape(sections * quarter, hidden), (((0,), (0,)), ((), ())),
                preferred_element_type=jnp.float32,
            )

        @pl.when(m == 0)
        def _():
            load_inp().wait()
            acc[...] = product()

        @pl.when(m > 0)
        def _():
            acc[...] += product()

    def block_of(d):
        at = exclusive_or(owner, d, bits) * block
        return pl.ds(pl.multiple_of(at, block), block)

    def reduce_stage(k):
        held = owners >> k

        def one(i, carry):
            h = held - 1 - i
            if k > 0:
                d = (1 << (k - 1)) + h * (1 << k)
                reduce_copy(d, k - 1).wait_recv()
                at = block_of(h * (1 << k))
                acc[at, :] = acc[at, :] + wrecv[d].astype(jnp.float32)
            if k < bits:
                @pl.when(lax.rem(h, 2) == 1)
                def _():
                    d = h * (1 << k)
                    wsend[d] = acc[block_of(d), :].astype(jnp.bfloat16)
                    reduce_copy(d, k).start()

            return carry

        with jax.named_scope(f"reduce{k}"):
            lax.fori_loop(0, held, one, 0)

    def send_ids():
        load_raw().wait()
        for target in range(owners):
            for slot in range(slots):
                f = (target * slots + slot) // row_split
                mine[target, :, slot : slot + 1, :] = raw[:, f : f + 1, :]
        pltpu.make_async_copy(mine.at[owner], places.at[owner], ids_recv).start()

        def send(k, carry):
            exchange_ids(lax.rem(owner + k, owners)).start()
            return carry

        lax.fori_loop(1, owners, send, 0)

    def gather_ids():
        pltpu.make_async_copy(places, places, ids_recv).wait()
        for m in range(micro_count):
            for source in range(owners):
                ids[m, :, source * quarter : (source + 1) * quarter] = places[
                    source, m
                ]
        tacc[...] = jnp.zeros_like(tacc)

    span = min(SPAN, owners * quarter)

    def tabulate(m):
        for j in range(per_micro):
            batch = arrived.at[m, :, pl.ds(j * PIECE, PIECE)]
            pltpu.make_async_copy(batch, batch, recv_sem.at[m * per_micro + j]).wait()

        def one(b, carry):
            sources = span // quarter
            rows = arrived[m, pl.ds(b * sources, sources)].reshape(span, slots * width)
            for slot in range(slots):
                row_block = lax.rem(owner * slots + slot, row_split)
                here = ids[m, slot : slot + 1, pl.ds(pl.multiple_of(b * span, span), span)]
                positions = lax.broadcasted_iota(jnp.int32, (TROWS, span), 0)
                onehot = (positions == here - row_block * TROWS).astype(jnp.float32)
                tacc[slot] += lax.dot_general(
                    onehot.astype(jnp.bfloat16), rows[:, slot * width : (slot + 1) * width],
                    (((1,), (0,)), ((), ())), preferred_element_type=jnp.float32,
                )
            return carry

        with jax.named_scope("tabulate"):
            lax.fori_loop(0, owners * quarter // span, one, 0)

    def share_tables():
        for target in range(sections):
            @pl.when(section != target)
            def _():
                tsend[target] = tacc[:, target * share : (target + 1) * share, :].astype(jnp.bfloat16)
                share_copy(target).start()

    with jax.named_scope("entry"):
        pl.semaphore_wait(barrier, owners - 1 + sections - 1)

    load_w().wait()

    @pl.when(section == last)
    def _():
        def first(m, carry):
            with jax.named_scope("head"):
                head(m)
            return carry

        def second(m, carry):
            with jax.named_scope("weigh"):
                weigh(m)
            return carry

        lax.fori_loop(0, micro_count, first, 0)
        lax.fori_loop(0, micro_count, second, 0)
        reduce_stage(0)
        send_ids()
        reduce_stage(1)

    @pl.when(section < last)
    def _():
        with jax.named_scope("turn"):
            wt[...] = w[...].T
        send_ids()
        for m in range(micro_count):
            load_pre(m).wait()

    lag = jnp.where((section == last) | (section == 0), 0, section * 2 + 1)
    most = last * 2 - 1

    def step(t, carry):
        @pl.when((section < last) & (t < chunks))
        def _():
            for i in range(subs):
                with jax.named_scope("chain"):
                    chain(t, i)

            @pl.when(lax.rem(t, per_micro) == per_micro - 1)
            def _():
                with jax.named_scope("weigh"):
                    weigh(t // per_micro)

            @pl.when(t == chunks - 1)
            def _():
                reduce_stage(0)

        p = t - lag

        @pl.when((p >= 0) & (p < chunks))
        def _():
            @pl.when(p == 0)
            def _():
                load_emb().wait()

            with jax.named_scope("pair"):
                pair(p)

        @pl.when((section < last) & (t == chunks))
        def _():
            reduce_stage(1)

        for k in range(2, bits + 1):
            @pl.when((section == last) & (t == 5 * (k - 1)))
            def _():
                reduce_stage(k)

        @pl.when(p == per_micro)
        def _():
            with jax.named_scope("ids"):
                gather_ids()

        @pl.when((p >= 2 * per_micro) & (lax.rem(p, per_micro) == 0) & (p < chunks))
        def _():
            tabulate(p // per_micro - 2)

        return carry

    lax.fori_loop(0, chunks + max(most, 5 * bits - chunks, 1), step, 0)

    @pl.when((section > 0) & (section < last))
    def _():
        reduce_stage(2)

    tabulate(micro_count - 2)
    tabulate(micro_count - 1)
    share_tables()

    @pl.when(section == 0)
    def _():
        reduce_stage(2)

    here = pl.ds(pl.multiple_of(section * share, share), share)
    total = tacc[:, here, :]
    with jax.named_scope("shared"):
        for k in range(1, sections):
            source = lax.rem(section + k, sections)
            pltpu.make_async_copy(trecv.at[source], trecv.at[source], trecv_sem.at[source]).wait()
            total = total + trecv[source].astype(jnp.float32)
        table_ref[...] = total

    @pl.when(section < last)
    def _():
        for k in range(3, bits + 1):
            reduce_stage(k)

    wg_ref[...] = acc[block_of(0), :]

    def drain_chain(u, carry):
        along(u).wait_send()
        return carry

    @pl.when(section > 0)
    def _():
        lax.fori_loop(0, chunks * subs, drain_chain, 0)

    def drain_hand(c, carry):
        sent = out_buf.at[c // per_micro, pl.ds(0, last), rows_of(lax.rem(c, per_micro))]
        pltpu.make_async_copy(sent, sent, hand_sem.at[c]).wait()
        return carry

    @pl.when(section == 0)
    def _():
        lax.fori_loop(0, chunks, drain_hand, 0)

    def drain_exchange(k, carry):
        target = lax.rem(owner + k, owners)
        sent = outgoing.at[target]
        pltpu.make_async_copy(sent, sent, send_sem.at[target]).wait()
        exchange_ids(target).wait_send()
        reduce_copy(k, 0).wait_send()
        return carry

    lax.fori_loop(1, owners, drain_exchange, 0)
    for k in range(1, sections):
        share_copy(lax.rem(section + k, sections)).wait_send()


def scale_kernel(grad_scale, wg_ref, table_ref, wg_out, table_out):
    wg_out[...] = wg_ref[...] * grad_scale
    table_out[...] = table_ref[...] * grad_scale


def whole_step(layer_w, layer_pre, cotangent, layer_in, embeddings, row_ids, slots, row_split):
    sections = lax.axis_size("section")
    owners = lax.axis_size("owner")
    micro_count, batch_rows, hidden = cotangent.shape
    quarter, features, width = embeddings.shape[1:]
    chunks = micro_count * (quarter // PIECE)
    share = TROWS // sections
    dims = (sections, owners, micro_count, quarter, features, width, slots, row_split)
    vmem = pl.BlockSpec(memory_space=pltpu.VMEM)
    anywhere = pl.BlockSpec(memory_space=pl.ANY)
    narrow, wide, whole = jnp.bfloat16, jnp.float32, jnp.int32
    split = (micro_count, sections, quarter, hidden)
    dma = pltpu.SemaphoreType.DMA
    return pl.pallas_call(
        functools.partial(step_kernel, dims),
        out_shape=(
            jax.ShapeDtypeStruct((hidden // owners, hidden), wide),
            jax.ShapeDtypeStruct((slots, share, width), wide),
        ),
        in_specs=[anywhere] * 6,
        out_specs=(vmem, vmem),
        scratch_shapes=[
            pltpu.VMEM((hidden, hidden), narrow),
            pltpu.VMEM((hidden, hidden), narrow),
            pltpu.VMEM(split, narrow),
            pltpu.VMEM(split, narrow),
            pltpu.VMEM((micro_count, batch_rows, hidden), narrow),
            pltpu.VMEM(embeddings.shape, narrow),
            pltpu.VMEM((micro_count, features, quarter), whole),
            pltpu.VMEM(split, narrow),
            pltpu.VMEM(split, narrow),
            pltpu.VMEM(split, narrow),
            pltpu.VMEM((chunks, PIECE, hidden), narrow),
            pltpu.VMEM((PIECE * features, 128), wide),
            pltpu.VMEM((PIECE * features, width), wide),
            pltpu.VMEM((owners, chunks, PIECE, slots * width), narrow),
            pltpu.VMEM((micro_count, owners, quarter, slots * width), narrow),
            pltpu.VMEM((owners, micro_count, slots, quarter), whole),
            pltpu.VMEM((owners, micro_count, slots, quarter), whole),
            pltpu.VMEM((micro_count, slots, owners * quarter), whole),
            pltpu.VMEM((hidden, hidden), wide),
            pltpu.VMEM((owners, hidden // owners, hidden), narrow),
            pltpu.VMEM((owners, hidden // owners, hidden), narrow),
            pltpu.VMEM((slots, TROWS, width), wide),
            pltpu.VMEM((sections, slots, share, width), narrow),
            pltpu.VMEM((sections, slots, share, width), narrow),
            dma(()),
            dma((micro_count,)),
            dma((micro_count,)),
            dma(()),
            dma(()),
            dma(()),
            dma((chunks * sections // GROUP,)),
            dma((chunks * sections // GROUP,)),
            dma((chunks,)),
            dma((chunks,)),
            dma((owners,)),
            dma((chunks,)),
            dma((owners,)),
            dma(()),
            dma((owners,)),
            dma((owners,)),
            dma((sections,)),
            dma((sections,)),
        ],
        compiler_params=pltpu.CompilerParams(
            collective_id=0, has_side_effects=True, vmem_limit_bytes=56 * 1024 * 1024
        ),
    )(
        layer_w, layer_pre.reshape(split), cotangent.reshape(split), layer_in, embeddings,
        jnp.swapaxes(row_ids, 1, 2),
    )


def per_device(weights, inputs, preact, cotangent, embeddings, row_ids):
    owners = lax.axis_size("owner")
    micro_count, batch_rows, hidden = cotangent.shape
    features = embeddings.shape[2]
    row_split = max(1, owners // features)
    slots = features * row_split // owners
    grad_scale = 1.0 / math.sqrt(micro_count * batch_rows * owners)
    weight_grad, table_grad = whole_step(
        weights[0], preact[0], cotangent, inputs[0], embeddings, row_ids, slots, row_split
    )
    vmem = pl.BlockSpec(memory_space=pltpu.VMEM)
    weight_grad, table_grad = pl.pallas_call(
        functools.partial(scale_kernel, grad_scale),
        out_shape=(
            jax.ShapeDtypeStruct(weight_grad.shape, jnp.float32),
            jax.ShapeDtypeStruct(table_grad.shape, jnp.float32),
        ),
        in_specs=[vmem, vmem],
        out_specs=(vmem, vmem),
    )(weight_grad, table_grad)
    return (weight_grad[None], table_grad)


def solution(mesh):
    return jax.shard_map(
        per_device,
        mesh=mesh,
        in_specs=(
            P("section", None, None),
            P("section", None, "owner", None),
            P("section", None, "owner", None),
            P(None, "owner", None),
            P(None, ("owner", "section"), None, None),
            P(None, ("owner", "section"), None),
        ),
        out_specs=(P("section", "owner", None), P("owner", "section", None)),
        check_vma=False,
    )
```

time: 107 us -> 99.6 us (0.931)
  the two profiles are of different devices: /device:TPU:2 before, /device:TPU:0 now
where the time goes in v1:
time: 99.6 us; the launch traced here: 98.7 us
  Pallas kernels  98.1 us (98%)
    pallas_call x1, Pallas kernels, whole_step(): pl.pallas_call(functools.partial(step_kernel, dims), out_shape=(jax.Shape...  96 us
    pallas_call x1, Pallas kernels, per_device(): pl.pallas_call(functools.partial(scale_kernel, grad_scale), out_shape=(ja...  2.03 us

profile of v1, /device:TPU:0, one launch (start us, length us, event | category | flops | bytes accessed | tf_op | source)
XLA Modules:
  0.0 98.7 jit_solution(436595402215938128)
XLA Ops:
  0.6 96.0 %shard_map.77 = (f32[128,1024]{1,0:T(8,128)}, f32[4,128,128]{2,1,0:T(8,128)}) custom-call(bf16[1024,1024]{1,0:T(8,128)(2,1)} %bitcast.6, bf16[4,4,64,1024]{3,2,1,0:T(8,128)(2,1)} %bitcast.7, bf16[4,4,64,1024]{3,2,1,0:T(8,128)(2,1)} %bitcast.8, bf16[4,256,1024]{2,1,0:T(8,128)(2,1)} %bitcast.9, bf16[4,64,32,128]{3,2,1,0:T(8,128)(2,1)} %emb_hbm.1, ...), custom_call_target="tpu_custom_call" | custom-call | tf_op jit(solution)/shard_map/pallas_call | solution.py:479
  96.7 2.0 %shard_map.78 = (f32[128,1024]{1,0:T(8,128)}, f32[4,128,128]{2,1,0:T(8,128)}) custom-call(f32[128,1024]{1,0:T(8,128)} %get-tuple-element.6.wg_ref, f32[4,128,128]{2,1,0:T(8,128)} %get-tuple-element.7.table_ref), custom_call_target="tpu_custom_call" | custom-call | tf_op jit(solution)/shard_map/pallas_call | solution.py:551

commit v2 on v1

--- a/solution.py
+++ b/solution.py
@@ -12,6 +12,7 @@
 PIECE = 16
 SPAN = 512
 GROUP = 2
+PROXY = 4
 
 
 def exclusive_or(a, b, bits):
@@ -24,9 +25,11 @@
 def step_kernel(
     dims, w_hbm, pre_hbm, cot_hbm, in_hbm, emb_hbm, ids_hbm, wg_ref, table_ref,
     w, wt, pre, cot, inp, emb, raw, slope, in_buf, out_buf, portion, square, pairs, outgoing,
-    arrived, mine, places, ids, acc, wsend, wrecv, tacc, tsend, trecv,
+    arrived, near, mine, places, near_places, ids, near_ids, acc, wsend, wrecv, tacc, nacc,
+    tsend, trecv, nsend, nrecv,
     w_sem, pre_sem, cot_sem, inp_sem, emb_sem, raw_sem, out_sem, in_sem, hand_sem, portion_sem,
-    send_sem, recv_sem, ids_send, ids_recv, wsend_sem, wrecv_sem, tsend_sem, trecv_sem,
+    send_sem, recv_sem, ids_send, ids_recv, near_send, near_ids_send, near_recv, wsend_sem, wrecv_sem,
+    tsend_sem, trecv_sem, nsend_sem, nrecv_sem,
 ):
     sections, owners, micro_count, quarter, features, width, slots, row_split = dims
     section = lax.axis_index("section")
@@ -40,6 +43,11 @@
     bits = owners.bit_length() - 1
     block = hidden // owners
     share = TROWS // sections
+    half = owners // 2
+    kept = slots // PROXY
+    direct = slots - kept
+    base_owner = owner // half * half
+    mirror = lax.rem(owner + half, owners)
 
     barrier = pltpu.get_barrier_semaphore()
     for k in range(1, sections):
@@ -53,6 +61,14 @@
             device_id_type=pl.DeviceIdType.MESH,
         )
 
+    if kept:
+        for k in range(1, sections):
+            pl.semaphore_signal(
+                barrier, inc=1,
+                device_id={"section": lax.rem(section + k, sections), "owner": mirror},
+                device_id_type=pl.DeviceIdType.MESH,
+            )
+
     def load_w():
         return pltpu.make_async_copy(w_hbm, w, w_sem)
 
@@ -109,13 +125,33 @@
             device_id_type=pl.DeviceIdType.MESH,
         )
 
-    def landing(c):
-        return arrived.at[c // per_micro, owner, rows_of(lax.rem(c, per_micro))]
-
-    def exchange(c, target):
-        return pltpu.make_async_remote_copy(
-            src_ref=outgoing.at[target, c], dst_ref=landing(c),
+    def lanes(count):
+        return pl.ds(0, count * width)
+
+    def landing(c, count):
+        return arrived.at[
+            c // per_micro, owner, rows_of(lax.rem(c, per_micro)), lanes(count)
+        ]
+
+    def near_landing(c):
+        return near.at[c // per_micro, owner - base_owner, rows_of(lax.rem(c, per_micro))]
+
+    def held_back(target, c):
+        opposite = lax.rem(target + half, owners)
+        return outgoing.at[opposite, c, :, pl.ds(direct * width, kept * width)]
+
+    def exchange(c, target, count):
+        return pltpu.make_async_remote_copy(
+            src_ref=outgoing.at[target, c, :, lanes(count)], dst_ref=landing(c, count),
             send_sem=send_sem.at[target], recv_sem=recv_sem.at[c],
+            device_id={"owner": target},
+            device_id_type=pl.DeviceIdType.MESH,
+        )
+
+    def exchange_near(c, target):
+        return pltpu.make_async_remote_copy(
+            src_ref=held_back(target, c), dst_ref=near_landing(c),
+            send_sem=near_send.at[target], recv_sem=recv_sem.at[c],
             device_id={"owner": target},
             device_id_type=pl.DeviceIdType.MESH,
         )
@@ -128,6 +164,15 @@
             device_id_type=pl.DeviceIdType.MESH,
         )
 
+    def near_ids_copy(target):
+        return pltpu.make_async_remote_copy(
+            src_ref=mine.at[lax.rem(target + half, owners)],
+            dst_ref=near_places.at[owner - base_owner],
+            send_sem=near_ids_send.at[target], recv_sem=near_recv,
+            device_id={"owner": target},
+            device_id_type=pl.DeviceIdType.MESH,
+        )
+
     def reduce_copy(d, k):
         return pltpu.make_async_remote_copy(
             src_ref=wsend.at[d], dst_ref=wrecv.at[d],
@@ -143,6 +188,17 @@
             device_id={"section": target},
             device_id_type=pl.DeviceIdType.MESH,
         )
+
+    def near_share(target):
+        return pltpu.make_async_remote_copy(
+            src_ref=nsend.at[target], dst_ref=nrecv.at[section],
+            send_sem=nsend_sem.at[target], recv_sem=nrecv_sem.at[section],
+            device_id={"section": target, "owner": mirror},
+            device_id_type=pl.DeviceIdType.MESH,
+        )
+
+    def neighbour(k):
+        return base_owner + lax.rem(owner - base_owner + k, half)
 
     def head(m):
         load_pre(m).wait()
@@ -214,12 +270,21 @@
                     pl.ds(f, PIECE, stride=features), :
                 ].astype(jnp.bfloat16)
 
-        def send(k, carry):
-            exchange(c, lax.rem(owner + k, owners)).start()
+        def send_far(k, carry):
+            exchange(c, lax.rem(neighbour(k) + half, owners), direct).start()
             return carry
 
-        lax.fori_loop(1, owners, send, 0)
-        pltpu.make_async_copy(outgoing.at[owner, c], landing(c), recv_sem.at[c]).start()
+        def send_close(k, carry):
+            exchange(c, neighbour(k), slots).start()
+            if kept:
+                exchange_near(c, neighbour(k)).start()
+            return carry
+
+        lax.fori_loop(0, half, send_far, 0)
+        lax.fori_loop(1, half, send_close, 0)
+        pltpu.make_async_copy(outgoing.at[owner, c], landing(c, slots), recv_sem.at[c]).start()
+        if kept:
+            pltpu.make_async_copy(held_back(owner, c), near_landing(c), recv_sem.at[c]).start()
 
     def weigh(m):
         def product():
@@ -241,11 +306,13 @@
         at = exclusive_or(owner, d, bits) * block
         return pl.ds(pl.multiple_of(at, block), block)
 
-    def reduce_stage(k):
+    def reduce_stage(k, part=None):
         held = owners >> k
+        top = held // 2 if part == 1 else held
+        count = held if part is None else held // 2
 
         def one(i, carry):
-            h = held - 1 - i
+            h = top - 1 - i
             if k > 0:
                 d = (1 << (k - 1)) + h * (1 << k)
                 reduce_copy(d, k - 1).wait_recv()
@@ -261,7 +328,7 @@
             return carry
 
         with jax.named_scope(f"reduce{k}"):
-            lax.fori_loop(0, held, one, 0)
+            lax.fori_loop(0, count, one, 0)
 
     def send_ids():
         load_raw().wait()
@@ -276,6 +343,15 @@
             return carry
 
         lax.fori_loop(1, owners, send, 0)
+        if kept:
+            own = near_places.at[owner - base_owner]
+            pltpu.make_async_copy(mine.at[mirror], own, near_recv).start()
+
+            def send_near(k, carry):
+                near_ids_copy(neighbour(k)).start()
+                return carry
+
+            lax.fori_loop(1, half, send_near, 0)
 
     def gather_ids():
         pltpu.make_async_copy(places, places, ids_recv).wait()
@@ -285,30 +361,49 @@
                     source, m
                 ]
         tacc[...] = jnp.zeros_like(tacc)
-
-    span = min(SPAN, owners * quarter)
+        if kept:
+            pltpu.make_async_copy(near_places, near_places, near_recv).wait()
+            for m in range(micro_count):
+                for source in range(half):
+                    near_ids[m, :, source * quarter : (source + 1) * quarter] = near_places[
+                        source, m
+                    ]
+            nacc[...] = jnp.zeros_like(nacc)
+
+    def collect(total, which, sources, first, rows, here, home):
+        span = min(SPAN, sources * quarter)
+        step = span // quarter
+
+        def one(b, carry):
+            at = first * quarter + b * span
+            block_rows = rows[0][rows[1], pl.ds(first + b * step, step)]
+            block_rows = block_rows.reshape(span, block_rows.shape[-1])
+            for slot, target, lane in which:
+                row_block = lax.rem(home * slots + slot, row_split)
+                named = here[0][here[1], slot : slot + 1, pl.ds(pl.multiple_of(at, span), span)]
+                positions = lax.broadcasted_iota(jnp.int32, (TROWS, span), 0)
+                onehot = (positions == named - row_block * TROWS).astype(jnp.float32)
+                total[target] += lax.dot_general(
+                    onehot.astype(jnp.bfloat16),
+                    block_rows[:, lane * width : (lane + 1) * width],
+                    (((1,), (0,)), ((), ())), preferred_element_type=jnp.float32,
+                )
+            return carry
+
+        lax.fori_loop(0, sources * quarter // span, one, 0)
 
     def tabulate(m):
         for j in range(per_micro):
             batch = arrived.at[m, :, pl.ds(j * PIECE, PIECE)]
             pltpu.make_async_copy(batch, batch, recv_sem.at[m * per_micro + j]).wait()
-
-        def one(b, carry):
-            sources = span // quarter
-            rows = arrived[m, pl.ds(b * sources, sources)].reshape(span, slots * width)
-            for slot in range(slots):
-                row_block = lax.rem(owner * slots + slot, row_split)
-                here = ids[m, slot : slot + 1, pl.ds(pl.multiple_of(b * span, span), span)]
-                positions = lax.broadcasted_iota(jnp.int32, (TROWS, span), 0)
-                onehot = (positions == here - row_block * TROWS).astype(jnp.float32)
-                tacc[slot] += lax.dot_general(
-                    onehot.astype(jnp.bfloat16), rows[:, slot * width : (slot + 1) * width],
-                    (((1,), (0,)), ((), ())), preferred_element_type=jnp.float32,
-                )
-            return carry
-
         with jax.named_scope("tabulate"):
-            lax.fori_loop(0, owners * quarter // span, one, 0)
+            everyone = [(slot, slot, slot) for slot in range(direct)]
+            collect(tacc, everyone, owners, 0, (arrived, m), (ids, m), owner)
+            if kept:
+                close = [(slot, slot, slot) for slot in range(direct, slots)]
+                collect(tacc, close, half, base_owner, (arrived, m), (ids, m), owner)
+                other = [(direct + i, i, i) for i in range(kept)]
+                collect(nacc, other, half, 0, (near, m), (near_ids, m), mirror)
 
     def share_tables():
         for target in range(sections):
@@ -317,8 +412,12 @@
                 tsend[target] = tacc[:, target * share : (target + 1) * share, :].astype(jnp.bfloat16)
                 share_copy(target).start()
 
+            if kept:
+                nsend[target] = nacc[:, target * share : (target + 1) * share, :].astype(jnp.bfloat16)
+                near_share(target).start()
+
     with jax.named_scope("entry"):
-        pl.semaphore_wait(barrier, owners - 1 + sections - 1)
+        pl.semaphore_wait(barrier, owners - 1 + (sections - 1) * (2 if kept else 1))
 
     load_w().wait()
 
@@ -380,7 +479,7 @@
 
         @pl.when((section < last) & (t == chunks))
         def _():
-            reduce_stage(1)
+            reduce_stage(1, 0)
 
         for k in range(2, bits + 1):
             @pl.when((section == last) & (t == 5 * (k - 1)))
@@ -398,11 +497,16 @@
 
         return carry
 
-    lax.fori_loop(0, chunks + max(most, 5 * bits - chunks, 1), step, 0)
+    rounds = jnp.where(section == 0, chunks + 1, chunks + max(most, 5 * bits - chunks, 1))
+    lax.fori_loop(0, rounds, step, 0)
+
+    @pl.when(section < last)
+    def _():
+        reduce_stage(1, 1)
 
     @pl.when((section > 0) & (section < last))
     def _():
-        reduce_stage(2)
+        reduce_stage(2, 0)
 
     tabulate(micro_count - 2)
     tabulate(micro_count - 1)
@@ -410,7 +514,15 @@
 
     @pl.when(section == 0)
     def _():
-        reduce_stage(2)
+        reduce_stage(2, 0)
+
+    @pl.when(section < last)
+    def _():
+        reduce_stage(2, 1)
+        for k in range(3, bits + 1):
+            reduce_stage(k)
+
+    wg_ref[...] = acc[block_of(0), :]
 
     here = pl.ds(pl.multiple_of(section * share, share), share)
     total = tacc[:, here, :]
@@ -420,13 +532,12 @@
             pltpu.make_async_copy(trecv.at[source], trecv.at[source], trecv_sem.at[source]).wait()
             total = total + trecv[source].astype(jnp.float32)
         table_ref[...] = total
-
-    @pl.when(section < last)
-    def _():
-        for k in range(3, bits + 1):
-            reduce_stage(k)
-
-    wg_ref[...] = acc[block_of(0), :]
+        if kept:
+            extra = jnp.zeros((kept, share, width), jnp.float32)
+            for source in range(sections):
+                pltpu.make_async_copy(nrecv.at[source], nrecv.at[source], nrecv_sem.at[source]).wait()
+                extra = extra + nrecv[source].astype(jnp.float32)
+            table_ref[direct:slots] = table_ref[direct:slots] + extra
 
     def drain_chain(u, carry):
         along(u).wait_send()
@@ -445,15 +556,34 @@
     def _():
         lax.fori_loop(0, chunks, drain_hand, 0)
 
-    def drain_exchange(k, carry):
-        target = lax.rem(owner + k, owners)
+    def drain_owner(k, carry):
+        exchange_ids(lax.rem(owner + k, owners)).wait_send()
+        reduce_copy(k, 0).wait_send()
+        return carry
+
+    lax.fori_loop(1, owners, drain_owner, 0)
+
+    def drain_far(k, carry):
+        target = lax.rem(neighbour(k) + half, owners)
+        sent = outgoing.at[target, :, :, lanes(direct)]
+        pltpu.make_async_copy(sent, sent, send_sem.at[target]).wait()
+        return carry
+
+    def drain_close(k, carry):
+        target = neighbour(k)
         sent = outgoing.at[target]
         pltpu.make_async_copy(sent, sent, send_sem.at[target]).wait()
-        exchange_ids(target).wait_send()
-        reduce_copy(k, 0).wait_send()
+        if kept:
+            sent = outgoing.at[target, :, :, pl.ds(direct * width, kept * width)]
+            pltpu.make_async_copy(sent, sent, near_send.at[target]).wait()
+            near_ids_copy(target).wait_send()
         return carry
 
-    lax.fori_loop(1, owners, drain_exchange, 0)
+    lax.fori_loop(0, half, drain_far, 0)
+    lax.fori_loop(1, half, drain_close, 0)
+    if kept:
+        for target in range(sections):
+            near_share(target).wait_send()
     for k in range(1, sections):
         share_copy(lax.rem(section + k, sections)).wait_send()
 
@@ -470,6 +600,7 @@
     quarter, features, width = embeddings.shape[1:]
     chunks = micro_count * (quarter // PIECE)
     share = TROWS // sections
+    kept = max(1, slots // PROXY)
     dims = (sections, owners, micro_count, quarter, features, width, slots, row_split)
     vmem = pl.BlockSpec(memory_space=pltpu.VMEM)
     anywhere = pl.BlockSpec(memory_space=pl.ANY)
@@ -500,15 +631,21 @@
             pltpu.VMEM((PIECE * features, width), wide),
             pltpu.VMEM((owners, chunks, PIECE, slots * width), narrow),
             pltpu.VMEM((micro_count, owners, quarter, slots * width), narrow),
+            pltpu.VMEM((micro_count, owners // 2, quarter, kept * width), narrow),
             pltpu.VMEM((owners, micro_count, slots, quarter), whole),
             pltpu.VMEM((owners, micro_count, slots, quarter), whole),
+            pltpu.VMEM((owners // 2, micro_count, slots, quarter), whole),
             pltpu.VMEM((micro_count, slots, owners * quarter), whole),
+            pltpu.VMEM((micro_count, slots, owners * quarter // 2), whole),
             pltpu.VMEM((hidden, hidden), wide),
             pltpu.VMEM((owners, hidden // owners, hidden), narrow),
             pltpu.VMEM((owners, hidden // owners, hidden), narrow),
             pltpu.VMEM((slots, TROWS, width), wide),
+            pltpu.VMEM((kept, TROWS, width), wide),
             pltpu.VMEM((sections, slots, share, width), narrow),
             pltpu.VMEM((sections, slots, share, width), narrow),
+            pltpu.VMEM((sections, kept, share, width), narrow),
+            pltpu.VMEM((sections, kept, share, width), narrow),
             dma(()),
             dma((micro_count,)),
             dma((micro_count,)),
@@ -525,6 +662,11 @@
             dma(()),
             dma((owners,)),
             dma((owners,)),
+            dma(()),
+            dma((owners,)),
+            dma((owners,)),
+            dma((sections,)),
+            dma((sections,)),
             dma((sections,)),
             dma((sections,)),
         ],

time: 99.6 us -> 96.8 us (0.972)
  Pallas kernels: 98.1 us -> 96.1 us
    pallas_call x1, Pallas kernels: 96 us -> 94 us  [whole_step(): pl.pallas_call(functools.partial(step_kernel, dims), out_shape=(jax.Shape...]
where the time goes in v2:
time: 96.8 us; the launch traced here: 96.7 us
  Pallas kernels  96.1 us (99%)
    pallas_call x1, Pallas kernels, whole_step(): pl.pallas_call(functools.partial(step_kernel, dims), out_shape=(jax.Shape...  94 us
    pallas_call x1, Pallas kernels, per_device(): pl.pallas_call(functools.partial(scale_kernel, grad_scale), out_shape=(ja...  2.03 us

profile of v2, /device:TPU:0, one launch (start us, length us, event | category | flops | bytes accessed | tf_op | source)
XLA Modules:
  0.0 96.7 jit_solution(15711636210207205228)
XLA Ops:
  0.6 94.0 %shard_map.77 = (f32[128,1024]{1,0:T(8,128)}, f32[4,128,128]{2,1,0:T(8,128)}) custom-call(bf16[1024,1024]{1,0:T(8,128)(2,1)} %bitcast.6, bf16[4,4,64,1024]{3,2,1,0:T(8,128)(2,1)} %bitcast.7, bf16[4,4,64,1024]{3,2,1,0:T(8,128)(2,1)} %bitcast.8, bf16[4,256,1024]{2,1,0:T(8,128)(2,1)} %bitcast.9, bf16[4,64,32,128]{3,2,1,0:T(8,128)(2,1)} %emb_hbm.1, ...), custom_call_target="tpu_custom_call" | custom-call | tf_op jit(solution)/shard_map/pallas_call | solution.py:610
  94.7 2.0 %shard_map.78 = (f32[128,1024]{1,0:T(8,128)}, f32[4,128,128]{2,1,0:T(8,128)}) custom-call(f32[128,1024]{1,0:T(8,128)} %get-tuple-element.6.wg_ref, f32[4,128,128]{2,1,0:T(8,128)} %get-tuple-element.7.table_ref), custom_call_target="tpu_custom_call" | custom-call | tf_op jit(solution)/shard_map/pallas_call | solution.py:693

commit v3 on v2

--- a/solution.py
+++ b/solution.py
@@ -13,6 +13,7 @@
 SPAN = 512
 GROUP = 2
 PROXY = 4
+SIDE = 4
 
 
 def exclusive_or(a, b, bits):
@@ -25,11 +26,12 @@
 def step_kernel(
     dims, w_hbm, pre_hbm, cot_hbm, in_hbm, emb_hbm, ids_hbm, wg_ref, table_ref,
     w, wt, pre, cot, inp, emb, raw, slope, in_buf, out_buf, portion, square, pairs, outgoing,
+    extra_out,
     arrived, near, mine, places, near_places, ids, near_ids, acc, wsend, wrecv, tacc, nacc,
-    tsend, trecv, nsend, nrecv,
+    tsend, trecv, nsend, nrecv, side_send, side_recv, sum_send, sum_recv,
     w_sem, pre_sem, cot_sem, inp_sem, emb_sem, raw_sem, out_sem, in_sem, hand_sem, portion_sem,
-    send_sem, recv_sem, ids_send, ids_recv, near_send, near_ids_send, near_recv, wsend_sem, wrecv_sem,
-    tsend_sem, trecv_sem, nsend_sem, nrecv_sem,
+    send_sem, recv_sem, close_sem, ids_send, ids_recv, near_send, near_ids_send, near_recv, wsend_sem, wrecv_sem,
+    tsend_sem, trecv_sem, nsend_sem, nrecv_sem, side_out, side_in, sum_out, sum_in, ready,
 ):
     sections, owners, micro_count, quarter, features, width, slots, row_split = dims
     section = lax.axis_index("section")
@@ -46,6 +48,7 @@
     half = owners // 2
     kept = slots // PROXY
     direct = slots - kept
+    main = hidden - hidden // SIDE // 128 * 128
     base_owner = owner // half * half
     mirror = lax.rem(owner + half, owners)
 
@@ -125,24 +128,15 @@
             device_id_type=pl.DeviceIdType.MESH,
         )
 
-    def lanes(count):
-        return pl.ds(0, count * width)
-
-    def landing(c, count):
-        return arrived.at[
-            c // per_micro, owner, rows_of(lax.rem(c, per_micro)), lanes(count)
-        ]
+    def landing(c):
+        return arrived.at[c // per_micro, owner, rows_of(lax.rem(c, per_micro))]
 
     def near_landing(c):
         return near.at[c // per_micro, owner - base_owner, rows_of(lax.rem(c, per_micro))]
 
-    def held_back(target, c):
-        opposite = lax.rem(target + half, owners)
-        return outgoing.at[opposite, c, :, pl.ds(direct * width, kept * width)]
-
-    def exchange(c, target, count):
-        return pltpu.make_async_remote_copy(
-            src_ref=outgoing.at[target, c, :, lanes(count)], dst_ref=landing(c, count),
+    def exchange(c, target):
+        return pltpu.make_async_remote_copy(
+            src_ref=outgoing.at[target, c], dst_ref=landing(c),
             send_sem=send_sem.at[target], recv_sem=recv_sem.at[c],
             device_id={"owner": target},
             device_id_type=pl.DeviceIdType.MESH,
@@ -150,8 +144,8 @@
 
     def exchange_near(c, target):
         return pltpu.make_async_remote_copy(
-            src_ref=held_back(target, c), dst_ref=near_landing(c),
-            send_sem=near_send.at[target], recv_sem=recv_sem.at[c],
+            src_ref=extra_out.at[target, c], dst_ref=near_landing(c),
+            send_sem=near_send.at[target], recv_sem=close_sem.at[c],
             device_id={"owner": target},
             device_id_type=pl.DeviceIdType.MESH,
         )
@@ -173,11 +167,28 @@
             device_id_type=pl.DeviceIdType.MESH,
         )
 
-    def reduce_copy(d, k):
-        return pltpu.make_async_remote_copy(
-            src_ref=wsend.at[d], dst_ref=wrecv.at[d],
+    def reduce_copy(d, k, count):
+        across = pl.ds(0, count)
+        return pltpu.make_async_remote_copy(
+            src_ref=wsend.at[d, :, across], dst_ref=wrecv.at[d, :, across],
             send_sem=wsend_sem.at[d], recv_sem=wrecv_sem.at[d],
             device_id={"owner": exclusive_or(owner, 1 << k, bits)},
+            device_id_type=pl.DeviceIdType.MESH,
+        )
+
+    def side_copy(h):
+        return pltpu.make_async_remote_copy(
+            src_ref=side_send.at[h], dst_ref=side_recv.at[section, h],
+            send_sem=side_out.at[h], recv_sem=side_in.at[section, h],
+            device_id={"section": last, "owner": exclusive_or(owner, 2 * h, bits)},
+            device_id_type=pl.DeviceIdType.MESH,
+        )
+
+    def sum_copy(target):
+        return pltpu.make_async_remote_copy(
+            src_ref=sum_send.at[target], dst_ref=sum_recv,
+            send_sem=sum_out.at[target], recv_sem=sum_in,
+            device_id={"section": target},
             device_id_type=pl.DeviceIdType.MESH,
         )
 
@@ -263,28 +274,37 @@
             both, emb[m, rows_of(j)], (((2,), (1,)), ((0,), (0,))),
             preferred_element_type=jnp.float32,
         ).reshape(PIECE * features, width)
+        def rows_for(f):
+            return pairs[pl.ds(f, PIECE, stride=features), :].astype(jnp.bfloat16)
+
         for target in range(owners):
-            for slot in range(slots):
+            for slot in range(direct):
                 f = (target * slots + slot) // row_split
-                outgoing[target, c, :, slot * width : (slot + 1) * width] = pairs[
-                    pl.ds(f, PIECE, stride=features), :
-                ].astype(jnp.bfloat16)
+                outgoing[target, c, :, slot * width : (slot + 1) * width] = rows_for(f)
+        opposite = [(target + half) % owners for target in range(owners)]
+        for target in range(owners):
+            for slot in range(kept):
+                f = (target * slots + direct + slot) // row_split
+                made = rows_for(f)
+                extra_out[target, c, :, slot * width : (slot + 1) * width] = made
+                lane = (kept + slot) * width
+                extra_out[opposite[target], c, :, lane : lane + width] = made
 
         def send_far(k, carry):
-            exchange(c, lax.rem(neighbour(k) + half, owners), direct).start()
+            exchange(c, lax.rem(neighbour(k) + half, owners)).start()
             return carry
 
         def send_close(k, carry):
-            exchange(c, neighbour(k), slots).start()
+            exchange(c, neighbour(k)).start()
             if kept:
                 exchange_near(c, neighbour(k)).start()
             return carry
 
         lax.fori_loop(0, half, send_far, 0)
         lax.fori_loop(1, half, send_close, 0)
-        pltpu.make_async_copy(outgoing.at[owner, c], landing(c, slots), recv_sem.at[c]).start()
+        pltpu.make_async_copy(outgoing.at[owner, c], landing(c), recv_sem.at[c]).start()
         if kept:
-            pltpu.make_async_copy(held_back(owner, c), near_landing(c), recv_sem.at[c]).start()
+            pltpu.make_async_copy(extra_out.at[owner, c], near_landing(c), close_sem.at[c]).start()
 
     def weigh(m):
         def product():
@@ -306,29 +326,56 @@
         at = exclusive_or(owner, d, bits) * block
         return pl.ds(pl.multiple_of(at, block), block)
 
-    def reduce_stage(k, part=None):
+    def send_block(d, k, count):
+        wsend[d, :, :count] = acc[block_of(d), :count].astype(jnp.bfloat16)
+        reduce_copy(d, k, count).start()
+
+    def reduce_stage(k, part=None, full=False):
         held = owners >> k
         top = held // 2 if part == 1 else held
         count = held if part is None else held // 2
+
+        def across(stage):
+            return hidden if full or stage == 0 else main
 
         def one(i, carry):
             h = top - 1 - i
             if k > 0:
                 d = (1 << (k - 1)) + h * (1 << k)
-                reduce_copy(d, k - 1).wait_recv()
+                come = across(k - 1)
+                reduce_copy(d, k - 1, come).wait_recv()
                 at = block_of(h * (1 << k))
-                acc[at, :] = acc[at, :] + wrecv[d].astype(jnp.float32)
+                acc[at, :come] = acc[at, :come] + wrecv[d, :, :come].astype(jnp.float32)
             if k < bits:
-                @pl.when(lax.rem(h, 2) == 1)
+                ahead = h >= held // 2 if k == 1 and not full else True
+                @pl.when((lax.rem(h, 2) == 1) & ahead)
                 def _():
-                    d = h * (1 << k)
-                    wsend[d] = acc[block_of(d), :].astype(jnp.bfloat16)
-                    reduce_copy(d, k).start()
+                    send_block(h * (1 << k), k, across(k))
+            if k == 1 and not full:
+                @pl.when(h > 0)
+                def _():
+                    side_send[h] = acc[block_of(h * 2), main:].astype(jnp.bfloat16)
+                    side_copy(h).start()
 
             return carry
 
         with jax.named_scope(f"reduce{k}"):
             lax.fori_loop(0, count, one, 0)
+
+    def send_rest():
+        with jax.named_scope("rest"):
+            for h in range(1, half // 2, 2):
+                send_block(2 * h, 1, main)
+
+    def side_sum(source):
+        with jax.named_scope("side"):
+            total = jnp.zeros((block, hidden - main), jnp.float32)
+            for h in range(1, half):
+                landed = side_recv.at[source, h]
+                pltpu.make_async_copy(landed, landed, side_in.at[source, h]).wait()
+                total = total + side_recv[source, h].astype(jnp.float32)
+            sum_send[source] = total.astype(jnp.bfloat16)
+            sum_copy(source).start()
 
     def send_ids():
         load_raw().wait()
@@ -370,13 +417,14 @@
                     ]
             nacc[...] = jnp.zeros_like(nacc)
 
-    def collect(total, which, sources, first, rows, here, home):
+    def collect(total, which, sources, first, rows, here, home, base=None):
         span = min(SPAN, sources * quarter)
         step = span // quarter
 
         def one(b, carry):
             at = first * quarter + b * span
-            block_rows = rows[0][rows[1], pl.ds(first + b * step, step)]
+            start = first if base is None else base
+            block_rows = rows[0][rows[1], pl.ds(start + b * step, step)]
             block_rows = block_rows.reshape(span, block_rows.shape[-1])
             for slot, target, lane in which:
                 row_block = lax.rem(home * slots + slot, row_split)
@@ -396,13 +444,16 @@
         for j in range(per_micro):
             batch = arrived.at[m, :, pl.ds(j * PIECE, PIECE)]
             pltpu.make_async_copy(batch, batch, recv_sem.at[m * per_micro + j]).wait()
+            if kept:
+                batch = near.at[m, :, pl.ds(j * PIECE, PIECE)]
+                pltpu.make_async_copy(batch, batch, close_sem.at[m * per_micro + j]).wait()
         with jax.named_scope("tabulate"):
             everyone = [(slot, slot, slot) for slot in range(direct)]
             collect(tacc, everyone, owners, 0, (arrived, m), (ids, m), owner)
             if kept:
-                close = [(slot, slot, slot) for slot in range(direct, slots)]
-                collect(tacc, close, half, base_owner, (arrived, m), (ids, m), owner)
-                other = [(direct + i, i, i) for i in range(kept)]
+                close = [(direct + i, direct + i, i) for i in range(kept)]
+                collect(tacc, close, half, base_owner, (near, m), (ids, m), owner, 0)
+                other = [(direct + i, i, kept + i) for i in range(kept)]
                 collect(nacc, other, half, 0, (near, m), (near_ids, m), mirror)
 
     def share_tables():
@@ -419,6 +470,14 @@
     with jax.named_scope("entry"):
         pl.semaphore_wait(barrier, owners - 1 + (sections - 1) * (2 if kept else 1))
 
+    @pl.when(section == last)
+    def _():
+        for target in range(last):
+            pl.semaphore_signal(
+                ready, inc=1, device_id={"section": target},
+                device_id_type=pl.DeviceIdType.MESH,
+            )
+
     load_w().wait()
 
     @pl.when(section == last)
@@ -435,9 +494,9 @@
 
         lax.fori_loop(0, micro_count, first, 0)
         lax.fori_loop(0, micro_count, second, 0)
-        reduce_stage(0)
+        reduce_stage(0, None, True)
         send_ids()
-        reduce_stage(1)
+        reduce_stage(1, None, True)
 
     @pl.when(section < last)
     def _():
@@ -446,6 +505,7 @@
         send_ids()
         for m in range(micro_count):
             load_pre(m).wait()
+        pl.semaphore_wait(ready, 1)
 
     lag = jnp.where((section == last) | (section == 0), 0, section * 2 + 1)
     most = last * 2 - 1
@@ -479,12 +539,12 @@
 
         @pl.when((section < last) & (t == chunks))
         def _():
-            reduce_stage(1, 0)
+            reduce_stage(1)
 
         for k in range(2, bits + 1):
             @pl.when((section == last) & (t == 5 * (k - 1)))
             def _():
-                reduce_stage(k)
+                reduce_stage(k, None, True)
 
         @pl.when(p == per_micro)
         def _():
@@ -499,10 +559,6 @@
 
     rounds = jnp.where(section == 0, chunks + 1, chunks + max(most, 5 * bits - chunks, 1))
     lax.fori_loop(0, rounds, step, 0)
-
-    @pl.when(section < last)
-    def _():
-        reduce_stage(1, 1)
 
     @pl.when((section > 0) & (section < last))
     def _():
@@ -512,15 +568,63 @@
     tabulate(micro_count - 1)
     share_tables()
 
+    @pl.when(section == last)
+    def _():
+        for source in range(last - 1, -1, -1):
+            side_sum(source)
+
+    @pl.when(section < last)
+    def _():
+        send_rest()
+
     @pl.when(section == 0)
     def _():
         reduce_stage(2, 0)
+
+    def drain_chain(u, carry):
+        along(u).wait_send()
+        return carry
+
+    @pl.when(section > 0)
+    def _():
+        lax.fori_loop(0, chunks * subs, drain_chain, 0)
+
+    def drain_hand(c, carry):
+        sent = out_buf.at[c // per_micro, pl.ds(0, last), rows_of(lax.rem(c, per_micro))]
+        pltpu.make_async_copy(sent, sent, hand_sem.at[c]).wait()
+        return carry
+
+    @pl.when(section == 0)
+    def _():
+        lax.fori_loop(0, chunks, drain_hand, 0)
+
+    def drain_far(k, carry):
+        target = lax.rem(neighbour(k) + half, owners)
+        sent = outgoing.at[target]
+        pltpu.make_async_copy(sent, sent, send_sem.at[target]).wait()
+        return carry
+
+    def drain_close(k, carry):
+        target = neighbour(k)
+        sent = outgoing.at[target]
+        pltpu.make_async_copy(sent, sent, send_sem.at[target]).wait()
+        if kept:
+            sent = extra_out.at[target]
+            pltpu.make_async_copy(sent, sent, near_send.at[target]).wait()
+            near_ids_copy(target).wait_send()
+        return carry
+
+    lax.fori_loop(0, half, drain_far, 0)
+    lax.fori_loop(1, half, drain_close, 0)
 
     @pl.when(section < last)
     def _():
         reduce_stage(2, 1)
         for k in range(3, bits + 1):
             reduce_stage(k)
+        with jax.named_scope("sum"):
+            pltpu.make_async_copy(sum_recv, sum_recv, sum_in).wait()
+            acc[block_of(0), main:] = acc[block_of(0), main:] + sum_recv[...].astype(jnp.float32)
 
     wg_ref[...] = acc[block_of(0), :]
 
@@ -539,48 +643,31 @@
                 extra = extra + nrecv[source].astype(jnp.float32)
             table_ref[direct:slots] = table_ref[direct:slots] + extra
 
-    def drain_chain(u, carry):
-        along(u).wait_send()
-        return carry
-
-    @pl.when(section > 0)
-    def _():
-        lax.fori_loop(0, chunks * subs, drain_chain, 0)
-
-    def drain_hand(c, carry):
-        sent = out_buf.at[c // per_micro, pl.ds(0, last), rows_of(lax.rem(c, per_micro))]
-        pltpu.make_async_copy(sent, sent, hand_sem.at[c]).wait()
-        return carry
-
-    @pl.when(section == 0)
-    def _():
-        lax.fori_loop(0, chunks, drain_hand, 0)
-
     def drain_owner(k, carry):
         exchange_ids(lax.rem(owner + k, owners)).wait_send()
-        reduce_copy(k, 0).wait_send()
         return carry
 
     lax.fori_loop(1, owners, drain_owner, 0)
 
-    def drain_far(k, carry):
-        target = lax.rem(neighbour(k) + half, owners)
-        sent = outgoing.at[target, :, :, lanes(direct)]
-        pltpu.make_async_copy(sent, sent, send_sem.at[target]).wait()
-        return carry
-
-    def drain_close(k, carry):
-        target = neighbour(k)
-        sent = outgoing.at[target]
-        pltpu.make_async_copy(sent, sent, send_sem.at[target]).wait()
-        if kept:
-            sent = outgoing.at[target, :, :, pl.ds(direct * width, kept * width)]
-            pltpu.make_async_copy(sent, sent, near_send.at[target]).wait()
-            near_ids_copy(target).wait_send()
-        return carry
-
-    lax.fori_loop(0, half, drain_far, 0)
-    lax.fori_loop(1, half, drain_close, 0)
+
+    def drain_blocks(full):
+        for k in range(bits):
+            for h in range(owners >> (k + 1)):
+                count = hidden if full or k == 0 else main
+                reduce_copy((1 << k) + h * (2 << k), k, count).wait_send()
+
+    @pl.when(section == last)
+    def _():
+        drain_blocks(True)
+        for target in range(last):
+            sum_copy(target).wait_send()
+
+    @pl.when(section < last)
+    def _():
+        drain_blocks(False)
+        for h in range(1, half):
+            side_copy(h).wait_send()
+
     if kept:
         for target in range(sections):
             near_share(target).wait_send()
@@ -600,10 +687,12 @@
     quarter, features, width = embeddings.shape[1:]
     chunks = micro_count * (quarter // PIECE)
     share = TROWS // sections
+    direct = slots - slots // PROXY
+    block, aside = hidden // owners, hidden // SIDE // 128 * 128
     kept = max(1, slots // PROXY)
     dims = (sections, owners, micro_count, quarter, features, width, slots, row_split)
     vmem = pl.BlockSpec(memory_space=pltpu.VMEM)
-    anywhere = pl.BlockSpec(memory_space=pl.ANY)
+    anywhere = pl.BlockSpec(memory_space=pltpu.HBM)
     narrow, wide, whole = jnp.bfloat16, jnp.float32, jnp.int32
     split = (micro_count, sections, quarter, hidden)
     dma = pltpu.SemaphoreType.DMA
@@ -629,9 +718,10 @@
             pltpu.VMEM((chunks, PIECE, hidden), narrow),
             pltpu.VMEM((PIECE * features, 128), wide),
             pltpu.VMEM((PIECE * features, width), wide),
-            pltpu.VMEM((owners, chunks, PIECE, slots * width), narrow),
-            pltpu.VMEM((micro_count, owners, quarter, slots * width), narrow),
-            pltpu.VMEM((micro_count, owners // 2, quarter, kept * width), narrow),
+            pltpu.VMEM((owners, chunks, PIECE, direct * width), narrow),
+            pltpu.VMEM((owners, chunks, PIECE, 2 * kept * width), narrow),
+            pltpu.VMEM((micro_count, owners, quarter, direct * width), narrow),
+            pltpu.VMEM((micro_count, owners // 2, quarter, 2 * kept * width), narrow),
             pltpu.VMEM((owners, micro_count, slots, quarter), whole),
             pltpu.VMEM((owners, micro_count, slots, quarter), whole),
             pltpu.VMEM((owners // 2, micro_count, slots, quarter), whole),
@@ -646,6 +736,10 @@
             pltpu.VMEM((sections, slots, share, width), narrow),
             pltpu.VMEM((sections, kept, share, width), narrow),
             pltpu.VMEM((sections, kept, share, width), narrow),
+            pltpu.VMEM((owners // 2, block, aside), narrow),
+            pltpu.VMEM((sections - 1, owners // 2, block, aside), narrow),
+            pltpu.VMEM((sections - 1, block, aside), narrow),
+            pltpu.VMEM((block, aside), narrow),
             dma(()),
             dma((micro_count,)),
             dma((micro_count,)),
@@ -658,6 +752,7 @@
             dma((chunks,)),
             dma((owners,)),
             dma((chunks,)),
+            dma((chunks,)),
             dma((owners,)),
             dma(()),
             dma((owners,)),
@@ -669,9 +764,14 @@
             dma((sections,)),
             dma((sections,)),
             dma((sections,)),
+            dma((owners // 2,)),
+            dma((sections - 1, owners // 2)),
+            dma((sections - 1,)),
+            dma(()),
+            pltpu.SemaphoreType.REGULAR,
         ],
         compiler_params=pltpu.CompilerParams(
-            collective_id=0, has_side_effects=True, vmem_limit_bytes=56 * 1024 * 1024
+            collective_id=0, has_side_effects=True, vmem_limit_bytes=54272 * 1024
         ),
     )(
         layer_w, layer_pre.reshape(split), cotangent.reshape(split), layer_in, embeddings,
@@ -698,6 +798,7 @@
         ),
         in_specs=[vmem, vmem],
         out_specs=(vmem, vmem),
+        compiler_params=pltpu.CompilerParams(vmem_limit_bytes=8 * 1024 * 1024),
     )(weight_grad, table_grad)
     return (weight_grad[None], table_grad)
 

time: 96.8 us -> 94.2 us (0.973)
  Pallas kernels: 96.1 us -> 92.4 us
    pallas_call x1, Pallas kernels: 94 us -> 91.4 us  [whole_step(): pl.pallas_call(functools.partial(step_kernel, dims), out_shape=(jax.Shape...]
    pallas_call x1, Pallas kernels: 2.03 us -> 0.94 us  [per_device(): pl.pallas_call(functools.partial(scale_kernel, grad_scale), out_shape=(ja...]
where the time goes in v3:
time: 94.2 us; the launch traced here: 93.9 us
  Pallas kernels  92.4 us (98%)
    pallas_call x1, Pallas kernels, whole_step(): pl.pallas_call(functools.partial(step_kernel, dims), out_shape=(jax.Shape...  91.4 us

profile of v3, /device:TPU:0, one launch (start us, length us, event | category | flops | bytes accessed | tf_op | source)
XLA Modules:
  0.0 93.9 jit_solution(9861709468627951405)
XLA Ops:
  0.6 0.0 copy-start
  0.6 0.8 copy-done
  1.5 91.4 %shard_map.77 = (f32[128,1024]{1,0:T(8,128)S(1)}, f32[4,128,128]{2,1,0:T(8,128)S(1)}) custom-call(bf16[1024,1024]{1,0:T(8,128)(2,1)} %bitcast.7, bf16[4,4,64,1024]{3,2,1,0:T(8,128)(2,1)} %bitcast.8, bf16[4,4,64,1024]{3,2,1,0:T(8,128)(2,1)} %bitcast.9, bf16[4,256,1024]{2,1,0:T(8,128)(2,1)} %bitcast.10, bf16[4,64,32,128]{3,2,1,0:T(8,128)(2,1)} %emb_hbm.1, ...), custom_call_target="tpu_custom_call" | custom-call | tf_op jit(solution)/shard_map/pallas_call | solution.py:699
  92.9 0.9 %shard_map.78 = (f32[128,1024]{1,0:T(8,128)}, f32[4,128,128]{2,1,0:T(8,128)}) custom-call(f32[128,1024]{1,0:T(8,128)S(1)} %get-tuple-element.6.wg_ref, f32[4,128,128]{2,1,0:T(8,128)S(1)} %get-tuple-element.7.table_ref), custom_call_target="tpu_custom_call" | custom-call | tf_op jit(solution)/shard_map/pallas_call | solution.py:793
Async XLA Ops:
  0.6 0.8 copy-start

commit v4 on v3

--- a/solution.py
+++ b/solution.py
@@ -775,7 +775,7 @@
         ),
     )(
         layer_w, layer_pre.reshape(split), cotangent.reshape(split), layer_in, embeddings,
-        jnp.swapaxes(row_ids, 1, 2),
+        pltpu.with_memory_space_constraint(jnp.swapaxes(row_ids, 1, 2), pltpu.HBM),
     )
 
 

time: 94.2 us -> 93.4 us (level)
  no operation moved by 1% of the time
where the time goes in v4:
time: 93.4 us; the launch traced here: 93.2 us
  Pallas kernels  92.5 us (99%)
    pallas_call x1, Pallas kernels, whole_step(): pl.pallas_call(functools.partial(step_kernel, dims), out_shape=(jax.Shape...  91.6 us

profile of v4, /device:TPU:0, one launch (start us, length us, event | category | flops | bytes accessed | tf_op | source)
XLA Modules:
  0.0 93.2 jit_solution(15325389157796224104)
XLA Ops:
  0.6 91.6 %shard_map.77 = (f32[128,1024]{1,0:T(8,128)S(1)}, f32[4,128,128]{2,1,0:T(8,128)S(1)}) custom-call(bf16[1024,1024]{1,0:T(8,128)(2,1)} %bitcast.6, bf16[4,4,64,1024]{3,2,1,0:T(8,128)(2,1)} %bitcast.7, bf16[4,4,64,1024]{3,2,1,0:T(8,128)(2,1)} %bitcast.8, bf16[4,256,1024]{2,1,0:T(8,128)(2,1)} %bitcast.9, bf16[4,64,32,128]{3,2,1,0:T(8,128)(2,1)} %emb_hbm.1, ...), custom_call_target="tpu_custom_call" | custom-call | tf_op jit(solution)/shard_map/pallas_call | solution.py:699
  92.2 0.9 %shard_map.78 = (f32[128,1024]{1,0:T(8,128)}, f32[4,128,128]{2,1,0:T(8,128)}) custom-call(f32[128,1024]{1,0:T(8,128)S(1)} %get-tuple-element.6.wg_ref, f32[4,128,128]{2,1,0:T(8,128)S(1)} %get-tuple-element.7.table_ref), custom_call_target="tpu_custom_call" | custom-call | tf_op jit(solution)/shard_map/pallas_call | solution.py:793

commit v5 on v4

--- a/solution.py
+++ b/solution.py
@@ -221,6 +221,7 @@
             preferred_element_type=jnp.float32,
         ).astype(jnp.bfloat16).reshape(sections, quarter, hidden)
 
+    def head_send(m):
         def send(i, carry):
             along(m * per_micro * subs + i).start()
             return carry
@@ -467,6 +468,11 @@
                 nsend[target] = nacc[:, target * share : (target + 1) * share, :].astype(jnp.bfloat16)
                 near_share(target).start()
 
+    @pl.when(section == last)
+    def _():
+        load_w().wait()
+        head(0)
+
     with jax.named_scope("entry"):
         pl.semaphore_wait(barrier, owners - 1 + (sections - 1) * (2 if kept else 1))
 
@@ -478,13 +484,14 @@
                 device_id_type=pl.DeviceIdType.MESH,
             )
 
-    load_w().wait()
-
     @pl.when(section == last)
     def _():
+        head_send(0)
+
         def first(m, carry):
             with jax.named_scope("head"):
                 head(m)
+                head_send(m)
             return carry
 
         def second(m, carry):
@@ -492,7 +499,7 @@
                 weigh(m)
             return carry
 
-        lax.fori_loop(0, micro_count, first, 0)
+        lax.fori_loop(1, micro_count, first, 0)
         lax.fori_loop(0, micro_count, second, 0)
         reduce_stage(0, None, True)
         send_ids()
@@ -500,6 +507,7 @@
 
     @pl.when(section < last)
     def _():
+        load_w().wait()
         with jax.named_scope("turn"):
             wt[...] = w[...].T
         send_ids()

time: 93.4 us -> 93.7 us (level)
  no operation moved by 1% of the time
where the time goes in v5:
time: 93.7 us; the launch traced here: 93.6 us
  Pallas kernels  92.9 us (99%)
    pallas_call x1, Pallas kernels, whole_step(): pl.pallas_call(functools.partial(step_kernel, dims), out_shape=(jax.Shape...  92 us

profile of v5, /device:TPU:0, one launch (start us, length us, event | category | flops | bytes accessed | tf_op | source)
XLA Modules:
  0.0 93.6 jit_solution(12363002007798772652)
XLA Ops:
  0.6 92.0 %shard_map.77 = (f32[128,1024]{1,0:T(8,128)S(1)}, f32[4,128,128]{2,1,0:T(8,128)S(1)}) custom-call(bf16[1024,1024]{1,0:T(8,128)(2,1)} %bitcast.6, bf16[4,4,64,1024]{3,2,1,0:T(8,128)(2,1)} %bitcast.7, bf16[4,4,64,1024]{3,2,1,0:T(8,128)(2,1)} %bitcast.8, bf16[4,256,1024]{2,1,0:T(8,128)(2,1)} %bitcast.9, bf16[4,64,32,128]{3,2,1,0:T(8,128)(2,1)} %emb_hbm.1, ...), custom_call_target="tpu_custom_call" | custom-call | tf_op jit(solution)/shard_map/pallas_call | solution.py:707
  92.6 0.9 %shard_map.78 = (f32[128,1024]{1,0:T(8,128)}, f32[4,128,128]{2,1,0:T(8,128)}) custom-call(f32[128,1024]{1,0:T(8,128)S(1)} %get-tuple-element.6.wg_ref, f32[4,128,128]{2,1,0:T(8,128)S(1)} %get-tuple-element.7.table_ref), custom_call_target="tpu_custom_call" | custom-call | tf_op jit(solution)/shard_map/pallas_call | solution.py:801
